TPU v7x, 32 devices: a whole 2x2x4 slice. The times are simulated.
32 devices in a mesh: groups: 2 (over x), gx: 16 (over z, y, core).
Axes of the slice: x: 2, y: 2, z: 4, core: 2. Of those that a mesh axis runs over, the one named last changes fastest.
Arguments:
- points: bfloat16 [32, 6, 1, 128, 512], P(('groups', 'gx')), parts along dimension 0, may hold values from -6 to 6
- order: int32 [32, 6, 1, 128], P(('groups', 'gx')), parts along dimension 0, may hold values from 0 to 127, each once within a row
- masks: int32 [32, 6, 1, 26], P(('groups', 'gx')), parts along dimension 0, may hold values 0 or 1
- counts: int32 [32, 6, 1], P('groups'), parts along dimension 0, may hold values from 1 to 128
- gain: float32 [512], replicated, may hold values from 0.5 to 1.5
- shift_bias: float32 [512], replicated, may hold values from -3 to 3
- w_qkv: bfloat16 [512, 1536], replicated, may hold values from -1.5 to 1.5
- w_out: bfloat16 [512, 512], replicated, may hold values from -0.25 to 0.25
Outputs:
- result: bfloat16 [32, 6, 1, 128, 512], P(('groups', 'gx')), parts along dimension 0
There are 2 independent parts, one for each index of `groups`. A program takes and returns all parts, laid end to end along the dimension named above; an argument that names none is the same for every part. Nothing has to cross between parts.
All inputs are finite; a program needn't handle non-finite values. No bound on the sum of `masks` on one device may be relied on, other than what follows from the above.
Results may differ from a plain program's by a relative error of at most 0.012.
Values may be sent and summed in bfloat16 or wider, within the bound.
A program may use at most 128 MiB of HBM per device.

v0:
```python
import jax
import jax.numpy as jnp
from jax import lax
from jax.sharding import PartitionSpec as P

HEADS = 8


neighbour_offsets = [(a, b, c) for a in (-1, 0, 1) for b in (-1, 0, 1) for c in (-1, 0, 1)]


def extended(value, sides, width):
    for axis, dim in sides:
        size, length = (lax.axis_size(axis), value.shape[dim])
        up = [(i, (i + 1) % size) for i in range(size - 1)]
        down = [(j, i) for i, j in up]
        last = lax.slice_in_dim(value, length - width, length, axis=dim)
        leading = lax.slice_in_dim(value, 0, width, axis=dim)
        before = lax.ppermute(last, axis, up)
        after = lax.ppermute(leading, axis, down)
        value = jnp.concatenate([before, value, after], axis=dim)
    return value


def column_of(a, b, c):
    index = 9 * (a + 1) + 3 * (b + 1) + (c + 1)
    return index if index < 13 else index - 1


def layer_norm(tiled, gain, shift_bias):
    values = tiled.astype(jnp.float32)
    mean = jnp.mean(values, axis=-1, keepdims=True)
    var = jnp.mean((values - mean) ** 2, axis=-1, keepdims=True)
    return ((values - mean) * lax.rsqrt(var + 1e-05) * gain + shift_bias).astype(jnp.bfloat16)


def reachable(offsets, by, bz):
    return [o for o in offsets if (by > 1 or o[1] == 0) and (bz > 1 or o[2] == 0)]


def collect_keys(slabs, counts_pad, masks, offsets, by, bz, p):
    positions = jnp.arange(p, dtype=jnp.int32)
    blocks = []
    valids = []
    for a, b, c in offsets:
        block = slabs[a + 1][1 + b : 1 + b + by, 1 + c : 1 + c + bz]
        near = counts_pad[a + 1, 1 + b : 1 + b + by, 1 + c : 1 + c + bz]
        valid = positions[None, None, :] < near[:, :, None]
        if (a, b, c) != (0, 0, 0):
            valid = valid & (masks[:, :, column_of(a, b, c)][:, :, None] == 1)
        blocks.append(block)
        valids.append(valid)
    width2 = blocks[0].shape[-1]
    keyvals = jnp.concatenate(blocks, axis=2).reshape(by * bz, -1, width2)
    valid = jnp.concatenate(valids, axis=2).reshape(by * bz, -1)
    return (keyvals, valid)


def head_major(query, keyval, heads):
    p, width = query.shape
    hd = width // heads
    qh = jnp.transpose(query.reshape(p, heads, hd), (1, 0, 2))
    kh = jnp.transpose(keyval[:, :width].reshape(-1, heads, hd), (1, 0, 2))
    vh = jnp.transpose(keyval[:, width:].reshape(-1, heads, hd), (1, 0, 2))
    return (qh, kh, vh)


def score_block(qh, kh, mask):
    scale = 1.0 / qh.shape[-1] ** 0.5
    scores = jnp.einsum("hqd,hkd->hqk", qh, kh, preferred_element_type=jnp.float32) * scale
    return jnp.where(mask[None, None, :], scores, -1e30)


def finish_block(scores, vh):
    top = jnp.max(scores, axis=-1, keepdims=True)
    probs = jnp.exp(scores - top)
    total = jnp.sum(probs, axis=-1, keepdims=True)
    accum = jnp.einsum(
        "hqk,hkd->hqd", probs.astype(jnp.bfloat16), vh, preferred_element_type=jnp.float32
    )
    out = accum / total
    heads, p, hd = out.shape
    return jnp.transpose(out, (1, 0, 2)).reshape(p, heads * hd)


def fetch_rims(operand):
    rims = extended(operand[None], (("gx", 0),), 1)
    return (rims[0], rims[2])


def pad_cross(slab):
    return jnp.pad(slab, ((1, 1), (1, 1), (0, 0), (0, 0)))


def shards(points, order, masks, counts, gain, shift_bias, w_qkv, w_out):
    _, by, bz, p, width = points.shape
    tiled = jnp.take_along_axis(points, order[..., None], axis=3)[0]
    normed = layer_norm(tiled, gain, shift_bias)
    qkv = jnp.dot(normed.reshape(-1, width), w_qkv, preferred_element_type=jnp.float32).astype(
        jnp.bfloat16
    )
    qkv = qkv.reshape(by, bz, p, 3 * width)
    queries = qkv[..., :width]
    keyvals = qkv[..., width:]
    place = lax.axis_index("gx")
    counts_pad = lax.dynamic_slice(
        jnp.pad(counts, 1), (place, jnp.int32(0), jnp.int32(0)), (3, by + 2, bz + 2)
    )
    own_masks = masks[0]
    w_keyvals = w_qkv[:, width:]
    flat_queries = queries.reshape(by * bz, p, width)

    def to_keyvals(rim):
        made = jnp.dot(rim.reshape(-1, width), w_keyvals, preferred_element_type=jnp.float32)
        return made.astype(jnp.bfloat16).reshape(by, bz, p, 2 * width)

    own_slab = pad_cross(keyvals)
    kept = reachable(neighbour_offsets, by, bz)
    below, above = fetch_rims(normed)
    slabs = (pad_cross(to_keyvals(below)), own_slab, pad_cross(to_keyvals(above)))
    gathered, valid = collect_keys(slabs, counts_pad, own_masks, kept, by, bz, p)

    def whole_block(operands):
        query, keyval, mask = operands
        qh, kh, vh = head_major(query, keyval, HEADS)
        return finish_block(score_block(qh, kh, mask), vh)

    attn = lax.map(whole_block, (flat_queries, gathered, valid))
    attn = attn.reshape(by, bz, p, width).astype(jnp.bfloat16)
    mixed = jnp.dot(attn.reshape(-1, width), w_out, preferred_element_type=jnp.float32).reshape(
        by, bz, p, width
    )
    mixed = tiled.astype(jnp.float32) + mixed
    own_counts = counts_pad[1, 1 : 1 + by, 1 : 1 + bz]
    live = jnp.arange(p, dtype=jnp.int32)[None, None, :] < own_counts[..., None]
    return jnp.where(live[..., None], mixed, 0.0).astype(jnp.bfloat16)[None]


def solution(mesh):
    placed = (
        P(("groups", "gx"), None, None, None, None),
        P(("groups", "gx"), None, None, None),
        P(("groups", "gx"), None, None, None),
        P("groups", None, None),
        P(),
        P(),
        P(),
        P(),
    )
    return jax.shard_map(
        shards,
        mesh=mesh,
        in_specs=placed,
        out_specs=P(("groups", "gx"), None, None, None, None),
        check_vma=False,
    )
```

profile of v0, /device:TPU:1, one launch (start us, length us, event | category | flops | bytes accessed | tf_op | source)
XLA Modules:
  0.0 97.5 jit_solution(1429662255774653734)
XLA Ops:
  0.8 2.3 %fusion.44 = (s32[6]{0:T(128)S(1)}, s32[6]{0:T(128)S(1)}, s32[6]{0:T(128)S(1)}, s32[6]{0:T(128)S(1)}, s32[6]{0:T(128)S(1)}, /*index=5*/s32[6]{0:T(128)S(1)}, s32[6]{0:T(128)S(1)}, s32[6]{0:T(128)S(1)}, s32[6]{0:T(128)S(1)}) fusion(s32[]{:T(128)S(6)} %add.132, s32[]{:T(128)S(6)} %add.125, s32[]{:T(128)S(6)} %add.120, s32[16,6,1]{0,2,1:T(1,128)} %param.13, ...), kind=kLoop, calls=%fused_computation.106 | loop fusion | bytes 620 | tf_op jit(solution)/shard_map/slice | solution.py:47
  3.8 5.5 %gather_fusion = bf16[768,512]{1,0:T(8,128)(2,1)S(1)} fusion(bf16[6,128,512]{2,1,0:T(8,128)(2,1)S(1)} %bitcast.81, s32[768]{0:T(1024)S(1)} %bitcast.84), kind=kCustom, calls=%fused_computation | custom fusion | bytes 1579008 | tf_op jit(solution)/shard_map/jit(take_along_axis)/gather | solution.py:97
  10.4 1.3 %add_convert_fusion = bf16[1,6,1,128,512]{4,3,1,2,0:T(8,128)(2,1)} fusion(f32[512]{0:T(512)S(1)} %copy-done.5, f32[512]{0:T(512)S(1)} %copy-done.6, f32[6,128]{1,0:T(8,128)S(1)} %get-tuple-element.74, f32[6,128]{1,0:T(8,128)S(1)} %get-tuple-element.77, bf16[1,6,1,128,512]{4,3,1,2,0:T(8,128)(2,1)S(1)} %bitcast.90, pred[6,128]{1,0:T(8,128)(4,1)S(1)} %get-tuple-element.79), kind=kLoop, calls=%fused_computation.34 | loop fusion | flops 2752512 | bytes 1583872 | tf_op jit(solution)/shard_map/convert_element_type | solution.py:34
  11.7 4.5 %collective-permute-start = (bf16[1,6,1,128,512]{4,3,1,2,0:T(8,128)(2,1)}, bf16[1,6,1,128,512]{4,3,1,2,0:T(8,128)(2,1)}, u32[]{:S(2)}, u32[]{:S(2)}) collective-permute-start(bf16[1,6,1,128,512]{4,3,1,2,0:T(8,128)(2,1)} %add_convert_fusion), channel_id=1, source_target_pairs={{0,1},{1,2},{2,3},{3,4},{4,5},{5,6},{6,7},{7,8},{8,9},{9,10},{10,1... | collective-permute-start | bytes 2359304 | tf_op jit(solution)/shard_map/ppermute | solution.py:19
  16.2 2.1 %collective-permute-start.1 = (bf16[1,6,1,128,512]{4,3,1,2,0:T(8,128)(2,1)}, bf16[1,6,1,128,512]{4,3,1,2,0:T(8,128)(2,1)}, u32[]{:S(2)}, u32[]{:S(2)}) collective-permute-start(bf16[1,6,1,128,512]{4,3,1,2,0:T(8,128)(2,1)} %add_convert_fusion), channel_id=1, source_target_pairs={{1,0},{2,1},{3,2},{4,3},{5,4},{6,5},{7,6},{8,7},{9,8},{10,9},{11,1... | collective-permute-start | bytes 2359304 | tf_op jit(solution)/shard_map/ppermute | solution.py:20
  18.3 3.0 %convolution_convert_fusion = bf16[768,1536]{1,0:T(8,128)(2,1)S(1)} fusion(bf16[512,1536]{1,0:T(8,128)(2,1)} %param.16, f32[512]{0:T(512)S(1)} %copy-done.5, f32[512]{0:T(512)S(1)} %copy-done.6, f32[768]{0:T(1024)S(1)} %get-tuple-element.75, f32[768]{0:T(1024)S(1)} %get-tuple-element.76, bf16[768,512]{1,0:T(8,128)(2,1)S(1)} %gather_fusion, ...), kind=kOutput, calls=%fused_computation.20 | convolution fusion | flops 1211891712 | bytes 4729600 | tf_op jit(solution)/shard_map/dot_general | solution.py:99
  21.3 1.4 %slice.127 = bf16[6,1,128,1024]{3,2,0,1:T(8,128)(2,1)} slice(bf16[6,1,128,1536]{3,2,0,1:T(8,128)(2,1)S(1)} %bitcast.93), slice={[0:6], [0:1], [0:128], [512:1536]} | slice | bytes 3145728 | tf_op jit(solution)/shard_map/slice | solution.py:104
  22.7 1.0 slice.126
  23.7 1.9 %copy.30 = bf16[6,1,128,1024]{2,3,0,1:T(8,128)(2,1)S(1)} copy(bf16[6,1,128,1024]{3,2,0,1:T(8,128)(2,1)} %slice.127) | data formatting | bytes 3145728
  25.6 2.3 %copy.29 = bf16[6,1,128,512]{2,3,0,1:T(8,128)(2,1)} copy(bf16[6,1,128,512]{3,2,0,1:T(8,128)(2,1)} %slice.126) | data formatting | bytes 1572864
  27.9 1.0 %compare_reduce_fusion = (pred[6]{0:T(512)(128)(4,1)S(1)}, pred[6]{0:T(512)(128)(4,1)S(1)}, pred[6]{0:T(512)(128)(4,1)S(1)}, pred[6]{0:T(512)(128)(4,1)S(1)}, pr...) fusion(s32[6,1,26]{2,1,0:T(1,128)S(1)} %bitcast.98), kind=kLoop, calls=%fused_computation.71 | loop fusion | flops 48 | bytes 240 | tf_op jit(solution)/shard_map/eq | solution.py:50
  29.7 4.2 %collective-permute-done = bf16[1,6,1,128,512]{4,3,1,2,0:T(8,128)(2,1)} collective-permute-done((bf16[1,6,1,128,512]{4,3,1,2,0:T(8,128)(2,1)}, bf16[1,6,1,128,512]{4,3,1,2,0:T(8,128)(2,1)}, u32[]{:S(2)}, u32[]{:S(2)}) %collective-permute-start) | collective-permute-done | bytes 786464 | tf_op jit(solution)/shard_map/ppermute | solution.py:19
  33.8 3.6 %convolution_convert_fusion.2 = bf16[768,1024]{1,0:T(8,128)(2,1)} fusion(bf16[768,512]{1,0:T(8,128)(2,1)} %bitcast.21, bf16[512,1536]{1,0:T(8,128)(2,1)} %param.16), kind=kOutput, calls=%fused_computation.24 | convolution fusion | flops 806092800 | bytes 3407872 | tf_op jit(solution)/shard_map/dot_general | solution.py:114
  37.4 2.6 %copy.19 = bf16[6,1,128,1024]{2,3,0,1:T(8,128)(2,1)} copy(bf16[6,1,128,1024]{3,2,0,1:T(8,128)(2,1)} %bitcast.95) | data formatting | bytes 3145728 | tf_op jit(solution)/shard_map/reshape | solution.py:115
  40.0 1.7 %fusion.14 = bf16[6,1,1152,1024]{2,3,0,1:T(8,128)(2,1)S(1)} fusion(bf16[6,1,128,1024]{2,3,0,1:T(8,128)(2,1)} %copy.19), kind=kLoop, calls=%fused_computation.27 | loop fusion | bytes 3145728
  43.8 1.1 %copy-done.7 = bf16[512,1536]{1,0:T(8,128)(2,1)S(1)} copy-done((bf16[512,1536]{1,0:T(8,128)(2,1)S(1)}, bf16[512,1536]{1,0:T(8,128)(2,1)}, u32[]{:S(2)}) %copy-start.7) | copy-done | bytes 1572888
  44.9 4.4 %convolution_convert_fusion.1 = bf16[768,1024]{1,0:T(8,128)(2,1)} fusion(bf16[768,512]{1,0:T(8,128)(2,1)} %bitcast.23, bf16[512,1536]{1,0:T(8,128)(2,1)S(1)} %copy-done.7), kind=kOutput, calls=%fused_computation.23 | convolution fusion | flops 806092800 | bytes 3407872 | tf_op jit(solution)/shard_map/dot_general | solution.py:114
  49.3 1.9 %copy.21 = bf16[6,1,128,1024]{2,3,0,1:T(8,128)(2,1)S(1)} copy(bf16[6,1,128,1024]{3,2,0,1:T(8,128)(2,1)} %bitcast.96) | data formatting | bytes 3145728 | tf_op jit(solution)/shard_map/reshape | solution.py:115
  51.2 1.3 %fusion.18 = bf16[6,1,1152,1024]{2,3,0,1:T(8,128)(2,1)} fusion(bf16[6,1,1152,1024]{2,3,0,1:T(8,128)(2,1)} %copy-done.2, bf16[6,1,128,1024]{2,3,0,1:T(8,128)(2,1)S(1)} %copy.21), kind=kLoop, calls=%fused_computation.31 | loop fusion | bytes 3145728
  52.5 1.4 %constant_dynamic-update-slice_fusion.10 = bf16[6,1,1152,1024]{2,3,0,1:T(8,128)(2,1)} fusion(bf16[6,1,1152,1024]{2,3,0,1:T(8,128)(2,1)} %fusion.18, bf16[6,1,128,1024]{2,3,0,1:T(8,128)(2,1)S(1)} %copy.21), kind=kLoop, calls=%fused_computation.67 | loop fusion | bytes 3145728
  53.9 1.3 %fusion.19 = bf16[6,1,1152,1024]{2,3,0,1:T(8,128)(2,1)} fusion(bf16[6,1,1152,1024]{2,3,0,1:T(8,128)(2,1)} %constant_dynamic-update-slice_fusion.10, bf16[6,1,128,1024]{2,3,0,1:T(8,128)(2,1)S(1)} %copy.21), kind=kLoop, calls=%fused_computation.32 | loop fusion | bytes 3145728 | tf_op jit(solution)/shard_map/concatenate | solution.py:54
  55.2 39.6 %while.10 = (s32[]{:T(128)}, bf16[6,128,512]{1,2,0:T(8,128)(2,1)}, pred[6,1152]{1,0:T(8,128)(4,1)S(1)}, bf16[6,128,512]{1,2,0:T(8,128)(2,1)}, bf16[6,1152,1024]{1,2,0:T(8,128)(2,1)}, /*index=5*/s32[]{:T(128)}) while((s32[]{:T(128)}, bf16[6,128,512]{1,2,0:T(8,128)(2,1)}, pred[6,1152]{1,0:T(8,128)(4,1)S(1)}, bf16[6,128,512]{1,2,0:T(8,128)(2,1)}, ...), condition=%wide.region_5.6_spmd, body=%wide.region_2.5_spmd.sunk | while | flops 310376448 | bytes 26763216 | solution.py:128
  55.2 1.9 %dynamic-slice_bitcast_fusion.2 = bf16[1152,1024]{0,1:T(8,128)(2,1)S(1)} fusion(bf16[6,1152,1024]{1,2,0:T(8,128)(2,1)} %get-tuple-element.135, s32[]{:T(128)} %get-tuple-element.125), kind=kLoop, calls=%fused_computation.8.clone.1 | loop fusion | bytes 4718596 | tf_op jit(solution)/shard_map/while/body/jit(dynamic_index_in_dim)/squeeze | solution.py:128
  57.3 0.9 constant_dynamic-slice_fusion.2
  59.2 0.9 fusion.79
  60.1 1.1 %fusion.80 = bf16[128,8,64]{0,2,1:T(8,128)(2,1)S(1)} fusion(bf16[8,1152,64]{1,2,0:T(8,128)(2,1)S(1)} %bitcast.82, f32[8,128,1152]{2,1,0:T(8,128)S(1)} %get-tuple-element.117, f32[8,128]{1,0:T(8,128)S(1)} %get-tuple-element.118, f32[128,8]{0,1:T(8,128)S(1)} %bitcast.97), kind=kOutput, calls=%fused_computation.10.clone.1 | convolution fusion | flops 153485312 | bytes 6037504 | tf_op jit(solution)/shard_map/while/body/eval_jaxpr/hqk,hkd->hqd/dot_general | solution.py:78
  61.9 1.8 %dynamic-slice_bitcast_fusion.2 = bf16[1152,1024]{0,1:T(8,128)(2,1)S(1)} fusion(bf16[6,1152,1024]{1,2,0:T(8,128)(2,1)} %get-tuple-element.135, s32[]{:T(128)} %get-tuple-element.125), kind=kLoop, calls=%fused_computation.8.clone.1 | loop fusion | bytes 4718596 | tf_op jit(solution)/shard_map/while/body/jit(dynamic_index_in_dim)/squeeze | solution.py:128
  63.9 0.9 constant_dynamic-slice_fusion.2
  65.8 0.9 fusion.79
  66.7 1.1 %fusion.80 = bf16[128,8,64]{0,2,1:T(8,128)(2,1)S(1)} fusion(bf16[8,1152,64]{1,2,0:T(8,128)(2,1)S(1)} %bitcast.82, f32[8,128,1152]{2,1,0:T(8,128)S(1)} %get-tuple-element.117, f32[8,128]{1,0:T(8,128)S(1)} %get-tuple-element.118, f32[128,8]{0,1:T(8,128)S(1)} %bitcast.97), kind=kOutput, calls=%fused_computation.10.clone.1 | convolution fusion | flops 153485312 | bytes 6037504 | tf_op jit(solution)/shard_map/while/body/eval_jaxpr/hqk,hkd->hqd/dot_general | solution.py:78
  68.5 1.8 %dynamic-slice_bitcast_fusion.2 = bf16[1152,1024]{0,1:T(8,128)(2,1)S(1)} fusion(bf16[6,1152,1024]{1,2,0:T(8,128)(2,1)} %get-tuple-element.135, s32[]{:T(128)} %get-tuple-element.125), kind=kLoop, calls=%fused_computation.8.clone.1 | loop fusion | bytes 4718596 | tf_op jit(solution)/shard_map/while/body/jit(dynamic_index_in_dim)/squeeze | solution.py:128
  70.5 0.9 constant_dynamic-slice_fusion.2
  71.5 0.9 fusion.78
  72.4 0.9 fusion.79
  73.3 1.1 %fusion.80 = bf16[128,8,64]{0,2,1:T(8,128)(2,1)S(1)} fusion(bf16[8,1152,64]{1,2,0:T(8,128)(2,1)S(1)} %bitcast.82, f32[8,128,1152]{2,1,0:T(8,128)S(1)} %get-tuple-element.117, f32[8,128]{1,0:T(8,128)S(1)} %get-tuple-element.118, f32[128,8]{0,1:T(8,128)S(1)} %bitcast.97), kind=kOutput, calls=%fused_computation.10.clone.1 | convolution fusion | flops 153485312 | bytes 6037504 | tf_op jit(solution)/shard_map/while/body/eval_jaxpr/hqk,hkd->hqd/dot_general | solution.py:78
  75.1 1.8 %dynamic-slice_bitcast_fusion.2 = bf16[1152,1024]{0,1:T(8,128)(2,1)S(1)} fusion(bf16[6,1152,1024]{1,2,0:T(8,128)(2,1)} %get-tuple-element.135, s32[]{:T(128)} %get-tuple-element.125), kind=kLoop, calls=%fused_computation.8.clone.1 | loop fusion | bytes 4718596 | tf_op jit(solution)/shard_map/while/body/jit(dynamic_index_in_dim)/squeeze | solution.py:128
  77.1 0.9 constant_dynamic-slice_fusion.2
  79.0 0.9 fusion.79
  79.9 1.1 %fusion.80 = bf16[128,8,64]{0,2,1:T(8,128)(2,1)S(1)} fusion(bf16[8,1152,64]{1,2,0:T(8,128)(2,1)S(1)} %bitcast.82, f32[8,128,1152]{2,1,0:T(8,128)S(1)} %get-tuple-element.117, f32[8,128]{1,0:T(8,128)S(1)} %get-tuple-element.118, f32[128,8]{0,1:T(8,128)S(1)} %bitcast.97), kind=kOutput, calls=%fused_computation.10.clone.1 | convolution fusion | flops 153485312 | bytes 6037504 | tf_op jit(solution)/shard_map/while/body/eval_jaxpr/hqk,hkd->hqd/dot_general | solution.py:78
  81.7 1.8 %dynamic-slice_bitcast_fusion.2 = bf16[1152,1024]{0,1:T(8,128)(2,1)S(1)} fusion(bf16[6,1152,1024]{1,2,0:T(8,128)(2,1)} %get-tuple-element.135, s32[]{:T(128)} %get-tuple-element.125), kind=kLoop, calls=%fused_computation.8.clone.1 | loop fusion | bytes 4718596 | tf_op jit(solution)/shard_map/while/body/jit(dynamic_index_in_dim)/squeeze | solution.py:128
  83.7 0.9 constant_dynamic-slice_fusion.2
  85.6 0.9 fusion.79
  86.5 1.1 %fusion.80 = bf16[128,8,64]{0,2,1:T(8,128)(2,1)S(1)} fusion(bf16[8,1152,64]{1,2,0:T(8,128)(2,1)S(1)} %bitcast.82, f32[8,128,1152]{2,1,0:T(8,128)S(1)} %get-tuple-element.117, f32[8,128]{1,0:T(8,128)S(1)} %get-tuple-element.118, f32[128,8]{0,1:T(8,128)S(1)} %bitcast.97), kind=kOutput, calls=%fused_computation.10.clone.1 | convolution fusion | flops 153485312 | bytes 6037504 | tf_op jit(solution)/shard_map/while/body/eval_jaxpr/hqk,hkd->hqd/dot_general | solution.py:78
  88.3 1.8 %dynamic-slice_bitcast_fusion.2 = bf16[1152,1024]{0,1:T(8,128)(2,1)S(1)} fusion(bf16[6,1152,1024]{1,2,0:T(8,128)(2,1)} %get-tuple-element.135, s32[]{:T(128)} %get-tuple-element.125), kind=kLoop, calls=%fused_computation.8.clone.1 | loop fusion | bytes 4718596 | tf_op jit(solution)/shard_map/while/body/jit(dynamic_index_in_dim)/squeeze | solution.py:128
  90.3 0.9 constant_dynamic-slice_fusion.2
  92.2 0.9 fusion.79
  93.1 1.1 %fusion.80 = bf16[128,8,64]{0,2,1:T(8,128)(2,1)S(1)} fusion(bf16[8,1152,64]{1,2,0:T(8,128)(2,1)S(1)} %bitcast.82, f32[8,128,1152]{2,1,0:T(8,128)S(1)} %get-tuple-element.117, f32[8,128]{1,0:T(8,128)S(1)} %get-tuple-element.118, f32[128,8]{0,1:T(8,128)S(1)} %bitcast.97), kind=kOutput, calls=%fused_computation.10.clone.1 | convolution fusion | flops 153485312 | bytes 6037504 | tf_op jit(solution)/shard_map/while/body/eval_jaxpr/hqk,hkd->hqd/dot_general | solution.py:78
  94.9 2.6 %fusion.20 = bf16[1,6,1,128,512]{4,3,2,1,0:T(8,128)(2,1)} fusion(bf16[6,128,512]{1,2,0:T(8,128)(2,1)} %get-tuple-element.32, bf16[6,128,512]{2,1,0:T(8,128)(2,1)S(1)} %bitcast.91, pred[6,128]{1,0:T(8,128)(4,1)S(1)} %get-tuple-element.79, pred[6,128]{1,0:T(8,128)(4,1)S(1)} %get-tuple-element.78, bf16[512,512]{1,0:T(8,128)(2,1)S(1)} %copy-done.8), kind=kOutput, calls=%fused_computation.36 | convolution fusion | flops 404619264 | bytes 2885120 | tf_op jit(solution)/shard_map/dot_general | solution.py:130
  (64 shorter events, 15.2 us)
Async XLA Ops:
  0.0 3.8 %copy-start = (bf16[1,6,1,128,512]{4,3,2,1,0:T(8,128)(2,1)S(1)}, bf16[1,6,1,128,512]{4,3,2,1,0:T(8,128)(2,1)}, u32[]{:S(2)}) copy-start(bf16[1,6,1,128,512]{4,3,2,1,0:T(8,128)(2,1)} %param.10) | copy-start | bytes 2359300
  9.3 1.0 %copy-start.5 = (f32[512]{0:T(512)S(1)}, f32[512]{0:T(512)}, u32[]{:S(2)}) copy-start(f32[512]{0:T(512)} %param.15) | copy-start | bytes 6148
  9.3 1.0 %copy-start.6 = (f32[512]{0:T(512)S(1)}, f32[512]{0:T(512)}, u32[]{:S(2)}) copy-start(f32[512]{0:T(512)} %param.14) | copy-start | bytes 6148
  9.3 9.0 %copy-start.4 = (s32[1,6,1,128]{3,2,1,0:T(1,128)S(1)}, s32[1,6,1,128]{3,2,1,0:T(1,128)}, u32[]{:S(2)}) copy-start(s32[1,6,1,128]{3,2,1,0:T(1,128)} %param.11) | copy-start | bytes 9220
  11.7 22.2 %collective-permute-start = (bf16[1,6,1,128,512]{4,3,1,2,0:T(8,128)(2,1)}, bf16[1,6,1,128,512]{4,3,1,2,0:T(8,128)(2,1)}, u32[]{:S(2)}, u32[]{:S(2)}) collective-permute-start(bf16[1,6,1,128,512]{4,3,1,2,0:T(8,128)(2,1)} %add_convert_fusion), channel_id=1, source_target_pairs={{0,1},{1,2},{2,3},{3,4},{4,5},{5,6},{6,7},{7,8},{8,9},{9,10},{10,1... | collective-permute-start | bytes 2359304 | tf_op jit(solution)/shard_map/ppermute | solution.py:19
  16.2 27.6 %collective-permute-start.1 = (bf16[1,6,1,128,512]{4,3,1,2,0:T(8,128)(2,1)}, bf16[1,6,1,128,512]{4,3,1,2,0:T(8,128)(2,1)}, u32[]{:S(2)}, u32[]{:S(2)}) collective-permute-start(bf16[1,6,1,128,512]{4,3,1,2,0:T(8,128)(2,1)} %add_convert_fusion), channel_id=1, source_target_pairs={{1,0},{2,1},{3,2},{4,3},{5,4},{6,5},{7,6},{8,7},{9,8},{10,9},{11,1... | collective-permute-start | bytes 2359304 | tf_op jit(solution)/shard_map/ppermute | solution.py:20
  25.6 2.3 %copy-start.3 = (s32[1,6,1,26]{3,2,1,0:T(1,128)S(1)}, s32[1,6,1,26]{3,2,1,0:T(1,128)}, u32[]{:S(2)}) copy-start(s32[1,6,1,26]{3,2,1,0:T(1,128)} %param.12) | copy-start | bytes 1876
  40.0 1.8 %copy-start.1 = (bf16[6,1,128,1024]{2,3,0,1:T(8,128)(2,1)S(1)}, bf16[6,1,128,1024]{2,3,0,1:T(8,128)(2,1)}, u32[]{:S(2)}) copy-start(bf16[6,1,128,1024]{2,3,0,1:T(8,128)(2,1)} %copy.19) | copy-start | bytes 4718596
  43.4 1.6 %copy-start.7 = (bf16[512,1536]{1,0:T(8,128)(2,1)S(1)}, bf16[512,1536]{1,0:T(8,128)(2,1)}, u32[]{:S(2)}) copy-start(bf16[512,1536]{1,0:T(8,128)(2,1)} %param.16) | copy-start | bytes 4718596
  43.8 5.5 %copy-start.2 = (bf16[6,1,1152,1024]{2,3,0,1:T(8,128)(2,1)}, bf16[6,1,1152,1024]{2,3,0,1:T(8,128)(2,1)S(1)}, u32[]{:S(2)}) copy-start(bf16[6,1,1152,1024]{2,3,0,1:T(8,128)(2,1)S(1)} %fusion.17) | copy-start | bytes 42467332
  55.2 39.7 %copy-start.8 = (bf16[512,512]{1,0:T(8,128)(2,1)S(1)}, bf16[512,512]{1,0:T(8,128)(2,1)}, u32[]{:S(2)}) copy-start(bf16[512,512]{1,0:T(8,128)(2,1)} %param.17) | copy-start | bytes 1572868
where the time goes:
time: 98.4 us; the launch traced here: 97.5 us
  local copies, waits for them, and re-layouts  49.7 us (51%)
  matrix products  25.5 us (26%)
  other arithmetic  11.1 us (11%)
  starting transfers between devices  6.62 us (7%)
  waiting for transfers between devices  4.19 us (4%)
    unnamed x28, local copies, waits for them, and re-layouts  11.8 us
    squeeze x6, local copies, waits for them, and re-layouts, shards(): attn = lax.map(whole_block, (flat_queries, gathered, valid))  11.1 us
    dot_general x2, matrix products, to_keyvals(): jnp.dot(rim.reshape(-1, width), w_keyvals, preferred_element_type=jnp.flo...  7.95 us
    dot_general x6, matrix products, finish_block(): jnp.einsum('hqk,hkd->hqd', probs.astype(jnp.bfloat16), vh, preferred_elem...  6.45 us
    dynamic_slice x12, local copies, waits for them, and re-layouts, shards(): attn = lax.map(whole_block, (flat_queries, gathered, valid))  5.74 us
    reduce_sum x6, other arithmetic, finish_block(): total = jnp.sum(probs, axis=-1, keepdims=True)  5.57 us
    dot_general x6, matrix products, score_block(): jnp.einsum('hqd,hkd->hqk', qh, kh, preferred_element_type=jnp.float32)  5.49 us
    gather x1, local copies, waits for them, and re-layouts, shards(): tiled = jnp.take_along_axis(points, order[..., None], axis=3)[0]  5.47 us
  transfers between devices with their start and end apart: 2, of which 1 were waited for; matrix products, arithmetic and copies ran while one was open for 22% of the time, Pallas kernels for 0%

commit v1 on v0

v1 whole, which is shorter than its diff:
```python
import functools

import jax
import jax.numpy as jnp
from jax import lax
from jax.experimental import pallas as pl
from jax.experimental.pallas import tpu as pltpu
from jax.sharding import PartitionSpec as P

HEADS = 8
TILE = 256
LANES = 128
NEG = -1e30


def column_of(a, b, c):
    index = 9 * (a + 1) + 3 * (b + 1) + (c + 1)
    return index if index < 13 else index - 1


def reach(by, bz):
    spans = [(b, c) for b in (0, -1, 1) for c in (0, -1, 1)]
    return [o for o in spans if (by > 1 or o[0] == 0) and (bz > 1 or o[1] == 0)]


def prepare(pts_ref, order_ref, gain, shift, normed_ref, tiled_ref, by, bz, p):
    def one(g, carry):
        row = order_ref[0, g // bz, pl.ds(g % bz, 1), :]
        pick = lax.broadcasted_iota(jnp.int32, (p, p), 0) == row
        pick = jnp.where(pick, 1.0, 0.0).astype(jnp.bfloat16)
        tiled = lax.dot_general(
            pick, pts_ref[g], (((0,), (0,)), ((), ())), preferred_element_type=jnp.float32
        )
        if tiled_ref is not None:
            tiled_ref[g] = tiled.astype(jnp.bfloat16)
        mean = jnp.mean(tiled, axis=-1, keepdims=True)
        away = tiled - mean
        var = jnp.mean(away * away, axis=-1, keepdims=True)
        normed = away * lax.rsqrt(var + 1e-05) * gain + shift
        rows = pl.ds(pl.multiple_of(g * p, p), p)
        normed_ref[rows, :] = normed.astype(jnp.bfloat16)
        return carry

    lax.fori_loop(0, by * bz, one, 0)


def project(normed_ref, w_ref, lo, hi, put):
    for col in range(lo, hi, TILE):
        part = jnp.dot(
            normed_ref[...], w_ref[:, col : col + TILE], preferred_element_type=jnp.float32
        )
        put(col, part)


def compact(slabs, masks_ref, counts_ref, kv_ref, keep_ref, table_ref, j, l, by, bz, p):
    near = reach(by, bz)
    off = jnp.int32(0)
    slot = 0
    for s, (kind, at, present) in enumerate(slabs):
        for b, c in near:
            jj, ll = j + b, l + c
            inside = (jj >= 0) & (jj < by) & (ll >= 0) & (ll < bz) & present
            jj, ll = jnp.clip(jj, 0, by - 1), jnp.clip(ll, 0, bz - 1)
            if kind is None:
                live = inside if (b, c) == (0, 0) else inside & (
                    masks_ref[0, j, l, column_of(0, b, c)] == 1
                )
            else:
                col = jnp.where(kind, column_of(1, b, c), column_of(-1, b, c))
                live = inside & (masks_ref[0, j, l, col] == 1)
            count = jnp.where(live, counts_ref[at, jj, ll], 0)
            table_ref[0, slot] = off
            table_ref[1, slot] = off + count
            start = pl.multiple_of(off, 16)
            source = pl.multiple_of((jj * bz + ll) * p, p)

            @pl.when(count > 0)
            def _():
                keep_ref[pl.ds(start, p), :] = kv_ref[s, pl.ds(source, p), :]

            off = off + ((count + 15) // 16) * 16
            slot += 1
    return off, slot


def attend(total, slots, table_ref, keep_ref, qs_ref, m_ref, l_ref, acc_ref, width, rows):
    groups = width // TILE

    def tile(t, carry):
        base = pl.multiple_of(t * TILE, TILE)
        place = base + lax.broadcasted_iota(jnp.int32, (1, TILE), 1)
        valid = jnp.zeros((1, TILE), jnp.int32)
        for n in range(slots):
            hit = (place >= table_ref[0, n]) & (place < table_ref[1, n])
            valid = jnp.where(hit, 1, valid)
        valid = valid == 1
        for g in range(groups):
            span = slice(g * rows, (g + 1) * rows)
            keys = keep_ref[pl.ds(base, TILE), g * TILE : (g + 1) * TILE]
            values = keep_ref[pl.ds(base, TILE), width + g * TILE : width + (g + 1) * TILE]
            s = lax.dot_general(
                qs_ref[span, :], keys, (((1,), (1,)), ((), ())), preferred_element_type=jnp.float32
            )
            s = jnp.where(valid, s, NEG)
            before = m_ref[span, :]
            top = jnp.maximum(before, jnp.max(s, axis=-1, keepdims=True))
            alpha = jnp.exp(before - top)
            parts = [jnp.exp(s[:, i : i + LANES] - top) for i in range(0, TILE, LANES)]
            l_ref[span, :] = l_ref[span, :] * alpha + sum(parts[1:], parts[0])
            m_ref[span, :] = top
            weights = jnp.concatenate(parts, axis=1).astype(jnp.bfloat16)
            out = jnp.dot(weights, values, preferred_element_type=jnp.float32)
            wide = jnp.concatenate([alpha] * (TILE // LANES), axis=1)
            acc_ref[span, :] = acc_ref[span, :] * wide + out
        return carry

    lax.fori_loop(0, (total + TILE - 1) // TILE, tile, 0)


def stack_queries(q_ref, g, qs_ref, p, hd):
    per = TILE // hd
    owner = lax.broadcasted_iota(jnp.int32, (p, TILE), 1) // hd
    for h in range(HEADS):
        lo = (h // per) * TILE
        part = q_ref[g, :, lo : lo + TILE].astype(jnp.float32)
        part = jnp.where(owner == h % per, part, 0.0)
        qs_ref[h * p : (h + 1) * p, :] = part.astype(jnp.bfloat16)


def near_kernel(dims, masks_ref, counts_ref, pts_ref, order_ref, pair_ref, pair_order_ref,
                gain_ref, shift_ref, w_ref, tiled_ref, q_ref, sum_ref, ml_ref,
                normed_ref, kv_ref, keep_ref, qs_ref, m_ref, l_ref, acc_ref, table_ref):
    by, bz, p, width, n = dims
    hd = width // HEADS
    per = TILE // hd
    me = lax.axis_index("gx")
    even = me % 2 == 0
    gain, shift = gain_ref[...], shift_ref[...]
    keep_ref[...] = jnp.zeros_like(keep_ref)

    prepare(pts_ref, order_ref, gain, shift, normed_ref, tiled_ref, by, bz, p)

    def put_q(col, part):
        part = part.astype(jnp.bfloat16) * jnp.bfloat16(1.0 / hd**0.5)
        q_ref[:, :, col : col + TILE] = part.reshape(by * bz, p, TILE)

    def put_kv(s):
        def put(col, part):
            kv_ref[s, :, col - width : col - width + TILE] = part.astype(jnp.bfloat16)

        return put

    project(normed_ref, w_ref, 0, width, put_q)
    project(normed_ref, w_ref, width, 3 * width, put_kv(0))
    prepare(pair_ref, pair_order_ref, gain, shift, normed_ref, None, by, bz, p)
    project(normed_ref, w_ref, width, 3 * width, put_kv(1))

    other = jnp.where(even, me + 1, me - 1)
    present = (other >= 0) & (other < n)
    slabs = [(None, me, True), (even, jnp.clip(other, 0, n - 1), present)]
    owner = lax.broadcasted_iota(jnp.int32, (p, TILE), 1) // hd
    lane = lax.broadcasted_iota(jnp.int32, (p, LANES), 1)

    def block(g, carry):
        j, l = g // bz, g % bz
        total, slots = compact(
            slabs, masks_ref, counts_ref, kv_ref, keep_ref, table_ref, j, l, by, bz, p
        )
        stack_queries(q_ref, g, qs_ref, p, hd)
        m_ref[...] = jnp.full_like(m_ref, NEG)
        l_ref[...] = jnp.zeros_like(l_ref)
        acc_ref[...] = jnp.zeros_like(acc_ref)
        attend(total, slots, table_ref, keep_ref, qs_ref, m_ref, l_ref, acc_ref, width, per * p)
        ml = jnp.zeros((p, LANES), jnp.float32)
        for h in range(HEADS):
            rows = slice(h * p, (h + 1) * p)
            ml = jnp.where(lane == h, m_ref[rows, :], ml)
            ml = jnp.where(lane == HEADS + h, jnp.sum(l_ref[rows, :], axis=-1, keepdims=True), ml)
        ml_ref[g] = ml
        for q in range(width // TILE):
            out = jnp.zeros((p, TILE), jnp.float32)
            for h in range(per):
                rows = slice((q * per + h) * p, (q * per + h + 1) * p)
                out = jnp.where(owner == h, acc_ref[rows, :], out)
            sum_ref[g, :, q * TILE : (q + 1) * TILE] = out
        return carry

    lax.fori_loop(0, by * bz, block, 0)


def far_kernel(dims, masks_ref, counts_ref, pts_ref, order_ref, gain_ref, shift_ref, w_ref,
               w_out_ref, tiled_ref, q_ref, sum_ref, ml_ref, out_ref,
               normed_ref, kv_ref, keep_ref, qs_ref, m_ref, l_ref, acc_ref, table_ref):
    by, bz, p, width, n = dims
    hd = width // HEADS
    per = TILE // hd
    me = lax.axis_index("gx")
    even = me % 2 == 0
    keep_ref[...] = jnp.zeros_like(keep_ref)
    prepare(pts_ref, order_ref, gain_ref[...], shift_ref[...], normed_ref, None, by, bz, p)

    def put(col, part):
        kv_ref[0, :, col - width : col - width + TILE] = part.astype(jnp.bfloat16)

    project(normed_ref, w_ref, width, 3 * width, put)
    other = jnp.where(even, me - 1, me + 1)
    present = (other >= 0) & (other < n)
    slabs = [(jnp.logical_not(even), jnp.clip(other, 0, n - 1), present)]
    owner = lax.broadcasted_iota(jnp.int32, (p, TILE), 1) // hd
    lane = lax.broadcasted_iota(jnp.int32, (p, LANES), 1)

    def block(g, carry):
        j, l = g // bz, g % bz
        total, slots = compact(
            slabs, masks_ref, counts_ref, kv_ref, keep_ref, table_ref, j, l, by, bz, p
        )
        stack_queries(q_ref, g, qs_ref, p, hd)
        ml = ml_ref[g]
        for h in range(HEADS):
            rows = slice(h * p, (h + 1) * p)
            m_ref[rows, :] = jnp.broadcast_to(ml[:, h : h + 1], (p, LANES))
            l_ref[rows, :] = jnp.where(lane == HEADS + h, ml, 0.0)
            lo = (h // per) * TILE
            acc_ref[rows, :] = sum_ref[g, :, lo : lo + TILE]
        attend(total, slots, table_ref, keep_ref, qs_ref, m_ref, l_ref, acc_ref, width, per * p)
        rows_out = pl.ds(pl.multiple_of(g * p, p), p)
        for q in range(width // TILE):
            out = jnp.zeros((p, TILE), jnp.float32)
            for h in range(per):
                rows = slice((q * per + h) * p, (q * per + h + 1) * p)
                scale = 1.0 / jnp.sum(l_ref[rows, :], axis=-1, keepdims=True)
                out = jnp.where(owner == h, acc_ref[rows, :] * scale, out)
            normed_ref[rows_out, q * TILE : (q + 1) * TILE] = out.astype(jnp.bfloat16)
        return carry

    lax.fori_loop(0, by * bz, block, 0)
    row = lax.broadcasted_iota(jnp.int32, (p, TILE), 0)
    for col in range(0, width, TILE):
        mixed = jnp.dot(
            normed_ref[...], w_out_ref[:, col : col + TILE], preferred_element_type=jnp.float32
        )
        for g in range(by * bz):
            part = mixed[g * p : (g + 1) * p] + tiled_ref[g, :, col : col + TILE].astype(jnp.float32)
            part = jnp.where(row < counts_ref[me, g // bz, g % bz], part, 0.0)
            out_ref[g, :, col : col + TILE] = part.astype(jnp.bfloat16)


def shards(points, order, masks, counts, gain, shift_bias, w_qkv, w_out):
    _, by, bz, p, width = points.shape
    n = lax.axis_size("gx")
    nb = by * bz
    dims = (by, bz, p, width, n)
    pairs = [e for i in range(0, n - 1, 2) for e in ((i, i + 1), (i + 1, i))]
    across = [e for i in range(1, n - 1, 2) for e in ((i, i + 1), (i + 1, i))]
    far_order = lax.ppermute(order, "gx", across)
    far = lax.ppermute(points, "gx", across)
    pair_order = lax.ppermute(order, "gx", pairs)
    pair = lax.ppermute(points, "gx", pairs)
    flat = lambda value: value.reshape(nb, p, width)
    gain, shift = gain.reshape(1, width), shift_bias.reshape(1, width)
    smem = pl.BlockSpec(memory_space=pltpu.SMEM)
    vmem = pl.BlockSpec(memory_space=pltpu.VMEM)
    slots = len(reach(by, bz))

    def scratch(slabs):
        cap = -(-slabs * slots * p // TILE) * TILE
        return [
            pltpu.VMEM((nb * p, width), jnp.bfloat16),
            pltpu.VMEM((slabs, nb * p, 2 * width), jnp.bfloat16),
            pltpu.VMEM((cap, 2 * width), jnp.bfloat16),
            pltpu.VMEM((HEADS * p, TILE), jnp.bfloat16),
            pltpu.VMEM((HEADS * p, LANES), jnp.float32),
            pltpu.VMEM((HEADS * p, LANES), jnp.float32),
            pltpu.VMEM((HEADS * p, TILE), jnp.float32),
            pltpu.SMEM((2, slabs * slots), jnp.int32),
        ]

    shape = jax.ShapeDtypeStruct
    tiled, q, total, ml = pl.pallas_call(
        functools.partial(near_kernel, dims),
        name="near",
        out_shape=[
            shape((nb, p, width), jnp.bfloat16),
            shape((nb, p, width), jnp.bfloat16),
            shape((nb, p, width), jnp.float32),
            shape((nb, p, LANES), jnp.float32),
        ],
        in_specs=[smem, smem] + [vmem] * 7,
        out_specs=[vmem] * 4,
        scratch_shapes=scratch(2),
        cost_estimate=pl.CostEstimate(
            flops=8 * nb * p * width * 5 * width, transcendentals=0, bytes_accessed=8 << 20
        ),
        compiler_params=pltpu.CompilerParams(vmem_limit_bytes=40 << 20),
    )(masks, counts, flat(points), order, flat(pair), pair_order, gain, shift, w_qkv)
    out = pl.pallas_call(
        functools.partial(far_kernel, dims),
        name="far",
        out_shape=shape((nb, p, width), jnp.bfloat16),
        in_specs=[smem, smem] + [vmem] * 10,
        out_specs=vmem,
        scratch_shapes=scratch(1),
        cost_estimate=pl.CostEstimate(
            flops=4 * nb * p * width * 3 * width, transcendentals=0, bytes_accessed=8 << 20
        ),
        compiler_params=pltpu.CompilerParams(vmem_limit_bytes=40 << 20),
    )(masks, counts, flat(far), far_order, gain, shift, w_qkv, w_out, tiled, q, total, ml)
    return out.reshape(points.shape)


def solution(mesh):
    placed = (
        P(("groups", "gx"), None, None, None, None),
        P(("groups", "gx"), None, None, None),
        P(("groups", "gx"), None, None, None),
        P("groups", None, None),
        P(),
        P(),
        P(),
        P(),
    )
    return jax.shard_map(
        shards,
        mesh=mesh,
        in_specs=placed,
        out_specs=P(("groups", "gx"), None, None, None, None),
        check_vma=False,
    )
```

time: 98.4 us -> 50.1 us (0.51); the launches traced: 97.5 us -> 50.6 us
  local copies, waits for them, and re-layouts: 49.7 us -> 6.07 us
  Pallas kernels: 0 us -> 36.3 us
  matrix products: 25.5 us -> 0 us
  other arithmetic: 11.1 us -> 0 us
  waiting for transfers between devices: 4.19 us -> 0.01 us
  starting transfers between devices: 6.62 us -> 8.11 us
    pallas_call x0 -> x2, Pallas kernels: none -> 36.3 us  [the longest x1 20.1 us: shards(): pl.pallas_call(functools.partial(near_kernel, dims), name='near', out_sha...]
    dot_general x16 -> x0, matrix products: 25.5 us -> none  [the longest x2 7.95 us: to_keyvals(): jnp.dot(rim.reshape(-1, width), w_keyvals, preferred_element_type=jnp.flo...]
    squeeze x6 -> x0, local copies, waits for them, and re-layouts: 11.1 us -> none  [shards(): attn = lax.map(whole_block, (flat_queries, gathered, valid))]
    reduce_sum x8 -> x0, other arithmetic: 6.53 us -> none  [the longest x6 5.57 us: finish_block(): total = jnp.sum(probs, axis=-1, keepdims=True)]
    dynamic_slice x12 -> x0, local copies, waits for them, and re-layouts: 5.74 us -> none  [shards(): attn = lax.map(whole_block, (flat_queries, gathered, valid))]
    slice x9 -> x0, local copies, waits for them, and re-layouts: 5.73 us -> none  [the longest x1 2.3 us: collect_keys(): near = counts_pad[a + 1, 1 + b:1 + b + by, 1 + c:1 + c + bz]]
    unnamed x28 -> x17, local copies, waits for them, and re-layouts: 11.8 us -> 6.07 us
    gather x1 -> x0, local copies, waits for them, and re-layouts: 5.47 us -> none  [shards(): tiled = jnp.take_along_axis(points, order[..., None], axis=3)[0]]
  transfers between devices with their start and end apart: 2 -> 4, of which waited for: 1 -> 0; matrix products, arithmetic and copies ran while one was open for 22% -> 2% of each run, Pallas kernels for 0% -> 40%
where the time goes in v1:
time: 50.1 us; the launch traced here: 50.6 us
  Pallas kernels  36.3 us (72%)
  starting transfers between devices  8.11 us (16%)
  local copies, waits for them, and re-layouts  6.07 us (12%)
    pallas_call x1, Pallas kernels, shards(): pl.pallas_call(functools.partial(near_kernel, dims), name='near', out_sha...  20.1 us
    pallas_call x1, Pallas kernels, shards(): pl.pallas_call(functools.partial(far_kernel, dims), name='far', out_shape...  16.2 us
    unnamed x17, local copies, waits for them, and re-layouts  6.07 us
    ppermute x1, starting transfers between devices, shards(): far = lax.ppermute(points, 'gx', across)  4.5 us
    ppermute x1, starting transfers between devices, shards(): far_order = lax.ppermute(order, 'gx', across)  3.52 us
  transfers between devices with their start and end apart: 4, of which 0 were waited for; matrix products, arithmetic and copies ran while one was open for 2% of the time, Pallas kernels for 40%

profile of v1, /device:TPU:1, one launch (start us, length us, event | category | flops | bytes accessed | tf_op | source)
XLA Modules:
  0.0 50.6 jit_solution(16337588663558846455)
XLA Ops:
  0.0 0.0 collective-permute-start.2
  0.0 4.5 %collective-permute-start = (bf16[1,6,1,128,512]{4,3,1,2,0:T(8,128)(2,1)}, bf16[1,6,1,128,512]{4,3,1,2,0:T(8,128)(2,1)S(1)}, u32[]{:S(2)}, u32[]{:S(2)}) collective-permute-start(bf16[1,6,1,128,512]{4,3,1,2,0:T(8,128)(2,1)} %bitcast.10), channel_id=1, source_target_pairs={{1,2},{2,1},{3,4},{4,3},{5,6},{6,5},{7,8},{8,7},{9,10},{10,9},{11,... | collective-permute-start | bytes 2359304 | tf_op jit(solution)/shard_map/ppermute | solution.py:256
  4.5 0.1 collective-permute-start.3
  4.6 3.5 %collective-permute-start.1 = (s32[1,6,1,128]{3,2,1,0:T(1,128)}, s32[1,6,1,128]{3,2,1,0:T(1,128)S(1)}, u32[]{:S(2)}, u32[]{:S(2)}) collective-permute-start(s32[1,6,1,128]{3,2,1,0:T(1,128)} %order_ref.1), channel_id=1, source_target_pairs={{1,2},{2,1},{3,4},{4,3},{5,6},{6,5},{7,8},{8,7},{9,10},{10,9},{11,... | collective-permute-start | bytes 9224 | tf_op jit(solution)/shard_map/ppermute | solution.py:255
  8.1 0.8 %copy.12.counts_ref = s32[16,6,1]{2,1,0:T(8,128)S(1)} copy(s32[16,6,1]{0,2,1:T(1,128)} %param.11) | data formatting | bytes 768 | tf_op args[3]
  8.9 0.0 collective-permute-done.3.pair_order_ref
  8.9 0.0 collective-permute-done.2
  9.0 0.0 copy-start
  9.0 1.4 %copy-done = bf16[512,1536]{1,0:T(8,128)(2,1)S(1)} copy-done((bf16[512,1536]{1,0:T(8,128)(2,1)S(1)}, bf16[512,1536]{1,0:T(8,128)(2,1)}, u32[]{:S(2)}) %copy-start) | copy-done | bytes 1572888
  10.4 0.0 copy-start.2
  10.4 1.1 %copy-done.2 = bf16[1,6,1,128,512]{4,3,2,1,0:T(8,128)(2,1)S(1)} copy-done((bf16[1,6,1,128,512]{4,3,2,1,0:T(8,128)(2,1)S(1)}, bf16[1,6,1,128,512]{4,3,2,1,0:T(8,128)(2,1)}, u32[]{:S(2)}) %copy-start.2) | copy-done | bytes 786456
  11.5 0.0 copy-start.4
  11.5 0.7 %copy-done.4 = s32[1,6,1,128]{3,2,1,0:T(1,128)S(1)} copy-done((s32[1,6,1,128]{3,2,1,0:T(1,128)S(1)}, s32[1,6,1,128]{3,2,1,0:T(1,128)}, u32[]{:S(2)}) %copy-start.4) | copy-done | bytes 3096
  12.2 0.0 copy-start.5
  12.2 0.7 %copy-done.5 = s32[1,6,1,26]{3,2,1,0:T(1,128)S(1)} copy-done((s32[1,6,1,26]{3,2,1,0:T(1,128)S(1)}, s32[1,6,1,26]{3,2,1,0:T(1,128)}, u32[]{:S(2)}) %copy-start.5) | copy-done | bytes 648
  12.9 0.0 copy-start.6
  12.9 0.7 %copy-done.6 = f32[512]{0:T(512)S(1)} copy-done((f32[512]{0:T(512)S(1)}, f32[512]{0:T(512)}, u32[]{:S(2)}) %copy-start.6) | copy-done | bytes 2072
  13.6 0.0 copy-start.7
  13.6 0.7 %copy-done.7 = f32[512]{0:T(512)S(1)} copy-done((f32[512]{0:T(512)S(1)}, f32[512]{0:T(512)}, u32[]{:S(2)}) %copy-start.7) | copy-done | bytes 2072
  14.2 0.0 copy-start.1
  14.2 0.0 copy-start.3
  14.2 20.1 %near.1 = (bf16[6,128,512]{2,1,0:T(8,128)(2,1)S(1)}, bf16[6,128,512]{2,1,0:T(8,128)(2,1)S(1)}, f32[6,128,512]{2,1,0:T(8,128)S(1)}, f32[6,128,128]{2,1,0:T(8,128)S(1)}) custom-call(s32[1,6,1,26]{3,2,1,0:T(1,128)S(1)} %copy-done.5, s32[16,6,1]{2,1,0:T(8,128)S(1)} %copy.12.counts_ref, bf16[6,128,512]{2,1,0:T(8,128)(2,1)S(1)} %bitcast.11, ...), custom_call_target="tpu_custom_call" | custom-call | flops 8053063680 | bytes 8388608 | tf_op jit(solution)/shard_map/near/pallas_call | solution.py:279
  34.4 0.0 collective-permute-done.1.order_ref
  34.4 0.0 collective-permute-done
  34.4 0.0 copy-done.1
  34.4 0.0 copy-done.3
  34.4 16.2 %far.1 = bf16[6,128,512]{2,1,0:T(8,128)(2,1)} custom-call(s32[1,6,1,26]{3,2,1,0:T(1,128)S(1)} %copy-done.5, s32[16,6,1]{2,1,0:T(8,128)S(1)} %copy.12.counts_ref, bf16[6,128,512]{2,1,0:T(8,128)(2,1)S(1)} %bitcast.12, s32[1,6,1,128]{3,2,1,0:T(1,128)S(1)} %collective-permute-done.1.order_ref, f32[1,512]{1,0:T(1,128)S(1)} %bitcast.15, f32[1,512]{1,0:T(1,128)S(1)} %bitcast.17, ...), custom_call_target="tpu_custom_call" | custom-call | flops 2415919104 | bytes 8388608 | tf_op jit(solution)/shard_map/far/pallas_call | solution.py:296
Async XLA Ops:
  0.0 8.9 %collective-permute-start.2 = (bf16[1,6,1,128,512]{4,3,1,2,0:T(8,128)(2,1)}, bf16[1,6,1,128,512]{4,3,1,2,0:T(8,128)(2,1)S(1)}, u32[]{:S(2)}, u32[]{:S(2)}) collective-permute-start(bf16[1,6,1,128,512]{4,3,1,2,0:T(8,128)(2,1)} %bitcast.9), channel_id=1, source_target_pairs={{0,1},{1,0},{2,3},{3,2},{4,5},{5,4},{6,7},{7,6},{8,9},{9,8},{10,11... | collective-permute-start | bytes 2359304 | tf_op jit(solution)/shard_map/ppermute | solution.py:258
  0.0 34.4 %collective-permute-start = (bf16[1,6,1,128,512]{4,3,1,2,0:T(8,128)(2,1)}, bf16[1,6,1,128,512]{4,3,1,2,0:T(8,128)(2,1)S(1)}, u32[]{:S(2)}, u32[]{:S(2)}) collective-permute-start(bf16[1,6,1,128,512]{4,3,1,2,0:T(8,128)(2,1)} %bitcast.10), channel_id=1, source_target_pairs={{1,2},{2,1},{3,4},{4,3},{5,6},{6,5},{7,8},{8,7},{9,10},{10,9},{11,... | collective-permute-start | bytes 2359304 | tf_op jit(solution)/shard_map/ppermute | solution.py:256
  4.5 4.4 %collective-permute-start.3 = (s32[1,6,1,128]{3,2,1,0:T(1,128)}, s32[1,6,1,128]{3,2,1,0:T(1,128)S(1)}, u32[]{:S(2)}, u32[]{:S(2)}) collective-permute-start(s32[1,6,1,128]{3,2,1,0:T(1,128)} %order_ref.1), channel_id=1, source_target_pairs={{0,1},{1,0},{2,3},{3,2},{4,5},{5,4},{6,7},{7,6},{8,9},{9,8},{10,11... | collective-permute-start | bytes 9224 | tf_op jit(solution)/shard_map/ppermute | solution.py:257
  4.6 29.8 %collective-permute-start.1 = (s32[1,6,1,128]{3,2,1,0:T(1,128)}, s32[1,6,1,128]{3,2,1,0:T(1,128)S(1)}, u32[]{:S(2)}, u32[]{:S(2)}) collective-permute-start(s32[1,6,1,128]{3,2,1,0:T(1,128)} %order_ref.1), channel_id=1, source_target_pairs={{1,2},{2,1},{3,4},{4,3},{5,6},{6,5},{7,8},{8,7},{9,10},{10,9},{11,... | collective-permute-start | bytes 9224 | tf_op jit(solution)/shard_map/ppermute | solution.py:255
  9.0 1.4 %copy-start = (bf16[512,1536]{1,0:T(8,128)(2,1)S(1)}, bf16[512,1536]{1,0:T(8,128)(2,1)}, u32[]{:S(2)}) copy-start(bf16[512,1536]{1,0:T(8,128)(2,1)} %w_ref.3) | copy-start | bytes 4718596
  10.4 1.1 %copy-start.2 = (bf16[1,6,1,128,512]{4,3,2,1,0:T(8,128)(2,1)S(1)}, bf16[1,6,1,128,512]{4,3,2,1,0:T(8,128)(2,1)}, u32[]{:S(2)}) copy-start(bf16[1,6,1,128,512]{4,3,2,1,0:T(8,128)(2,1)} %param.8) | copy-start | bytes 2359300
  11.5 0.7 %copy-start.4 = (s32[1,6,1,128]{3,2,1,0:T(1,128)S(1)}, s32[1,6,1,128]{3,2,1,0:T(1,128)}, u32[]{:S(2)}) copy-start(s32[1,6,1,128]{3,2,1,0:T(1,128)} %order_ref.1) | copy-start | bytes 9220
  12.2 0.7 %copy-start.5 = (s32[1,6,1,26]{3,2,1,0:T(1,128)S(1)}, s32[1,6,1,26]{3,2,1,0:T(1,128)}, u32[]{:S(2)}) copy-start(s32[1,6,1,26]{3,2,1,0:T(1,128)} %masks_ref.3) | copy-start | bytes 1876
  12.9 0.7 %copy-start.6 = (f32[512]{0:T(512)S(1)}, f32[512]{0:T(512)}, u32[]{:S(2)}) copy-start(f32[512]{0:T(512)} %param.12) | copy-start | bytes 6148
  13.6 0.7 %copy-start.7 = (f32[512]{0:T(512)S(1)}, f32[512]{0:T(512)}, u32[]{:S(2)}) copy-start(f32[512]{0:T(512)} %param.13) | copy-start | bytes 6148
  14.2 20.2 %copy-start.1 = (bf16[512,1536]{1,0:T(8,128)(2,1)S(1)}, bf16[512,1536]{1,0:T(8,128)(2,1)}, u32[]{:S(2)}) copy-start(bf16[512,1536]{1,0:T(8,128)(2,1)} %w_ref.3) | copy-start | bytes 4718596
  14.2 20.2 %copy-start.3 = (bf16[512,512]{1,0:T(8,128)(2,1)S(1)}, bf16[512,512]{1,0:T(8,128)(2,1)}, u32[]{:S(2)}) copy-start(bf16[512,512]{1,0:T(8,128)(2,1)} %w_out_ref.1) | copy-start | bytes 1572868
